TPU v7x, 32 devices: a whole 2x2x4 slice. The times are simulated.
32 devices in a mesh: date: 4 (over y, x), pix: 8 (over z, core).
Axes of the slice: x: 2, y: 2, z: 4, core: 2. Of those that a mesh axis runs over, the one named last changes fastest.
Arguments:
- stack: bfloat16 [64, 7, 64, 1024], P('date', None, None, 'pix'), may hold values from -8 to 8
- quality: int32 [64, 64, 1024], P('date', None, 'pix'), may hold values from 0 to 1073741823
- days: int32 [64], P('date'), may hold values from 8 to 1536, as said below
Outputs:
- coef: float32 [7, 8, 64, 1024], P(None, None, 'pix', 'date')
- score: float32 [7, 64, 1024], P(None, 'pix', 'date')
Inputs may be any that keep to these rules, and one draw needn't show every extreme that they name: `days`: strictly increasing.
All inputs are finite; a program needn't handle non-finite values.
Results may differ from a plain program's by a relative error of at most 0.0003.
Values may be sent and summed in bfloat16 or wider, within the bound.
A program may use at most 256 MiB of HBM per device.

v0:
```python
import jax
import jax.numpy as jnp
from jax import lax
from jax.sharding import PartitionSpec as P

RIDGE_TERM = 1.0
PAIR_LIST = [(first, second) for first in range(8) for second in range(first, 8)]


def pair_number(first, second):
    return PAIR_LIST.index((min(first, second), max(first, second)))


def design_matrix(days):
    moment_t = days.astype(jnp.float32)
    columns = [jnp.ones_like(moment_t), (moment_t - 512.0) / 512.0]
    for order in range(1, 4):
        phase = 2.0 * jnp.pi * order * moment_t / 365.25
        columns.append(jnp.cos(phase))
        columns.append(jnp.sin(phase))
    return jnp.stack(columns, 1)


def weights(quality):
    cloud = jnp.bitwise_and(jnp.right_shift(quality, 3), 1)
    level = jnp.bitwise_and(jnp.right_shift(quality, 8), 3)
    return (1 - cloud).astype(jnp.float32) / (1.0 + level.astype(jnp.float32))


def pair_products(design):
    return jnp.stack([design[:, first] * design[:, second] for first, second in PAIR_LIST], 1)


def chol_solve(gram, moment):
    lower = {}
    for first in range(8):
        for second in range(first + 1):
            total = gram[pair_number(first, second)]
            if first == second:
                total = total + RIDGE_TERM
            for inner in range(second):
                total = total - lower[first, inner] * lower[second, inner]
            if first == second:
                lower[first, first] = jnp.sqrt(total)
            else:
                lower[first, second] = total / lower[second, second]
    forward = []
    for first in range(8):
        total = moment[first]
        for inner in range(first):
            total = total - lower[first, inner][None, :] * forward[inner]
        forward.append(total / lower[first, first][None, :])
    backward = [None] * 8
    for first in range(7, -1, -1):
        total = forward[first]
        for inner in range(first + 1, 8):
            total = total - lower[inner, first][None, :] * backward[inner]
        backward[first] = total / lower[first, first][None, :]
    return jnp.stack(backward, 0)


def local(stack, quality, days):
    high = lax.Precision.HIGHEST
    bands = stack.shape[1]
    local_dates, all_rows, arrive_cols = (stack.shape[0], stack.shape[2], stack.shape[3])
    arrive_pixels = all_rows * arrive_cols
    design = design_matrix(days)
    weight = weights(quality).reshape(local_dates, arrive_pixels)
    samples = stack.reshape(local_dates, bands, arrive_pixels).astype(jnp.float32)
    gram_part = jnp.dot(pair_products(design).T, weight, precision=high)
    weighted = weight[:, None, :] * samples
    moment_part = jnp.dot(
        design.T, weighted.reshape(local_dates, bands * arrive_pixels), precision=high
    )
    square_part = jnp.sum(weighted * samples, 0)
    weight_part = jnp.sum(weight, 0)[None, :]
    stacked = jnp.concatenate(
        [gram_part, moment_part.reshape(8 * bands, arrive_pixels), square_part, weight_part], 0
    )
    stacked = stacked.reshape(stacked.shape[0], all_rows, arrive_cols)
    spread = lax.all_to_all(stacked, "pix", split_axis=1, concat_axis=2, tiled=True)
    summed = lax.psum_scatter(spread, "date", scatter_dimension=2, tiled=True)
    row_count, col_count = (summed.shape[1], summed.shape[2])
    pixels = row_count * col_count
    summed = summed.reshape(summed.shape[0], pixels)
    gram = summed[:36]
    moment = summed[36 : 36 + 8 * bands].reshape(8, bands, pixels)
    squares = summed[36 + 8 * bands : 36 + 9 * bands]
    wsum = summed[36 + 9 * bands]
    coef_flat = chol_solve(gram, moment)
    ssr = squares - 2.0 * jnp.sum(coef_flat * moment, 0)
    for first in range(8):
        for second in range(8):
            ssr = (
                ssr
                + gram[pair_number(first, second)][None, :] * coef_flat[first] * coef_flat[second]
            )
    total_ssr, total_weight = lax.psum((jnp.sum(ssr, 1), jnp.sum(wsum)), ("date", "pix"))
    sigma2 = total_ssr / total_weight
    score = jnp.sqrt(ssr / (wsum[None, :] + 1.0)) / jnp.sqrt(sigma2)[:, None]
    coef = jnp.transpose(coef_flat.reshape(8, bands, row_count, col_count), (1, 0, 2, 3))
    return (coef, score.reshape(bands, row_count, col_count))


def solution(mesh):
    return jax.shard_map(
        local,
        mesh=mesh,
        in_specs=(P("date", None, None, "pix"), P("date", None, "pix"), P("date")),
        out_specs=(P(None, None, "pix", "date"), P(None, "pix", "date")),
        check_vma=False,
    )
```

profile of v0, /device:TPU:0, one launch (start us, length us, event | category | flops | bytes accessed | tf_op | source)
XLA Modules:
  0.0 227.7 jit_solution(3004523274341131072)
XLA Ops:
  7.2 1.2 fusion.103
  8.5 2.0 fusion
  12.0 3.9 %copy.189 = f32[2,8,7,8192]{3,1,2,0:T(8,128)} copy(f32[2,8,7,8192]{3,2,1,0:T(8,128)S(1)} %bitcast.504) | data formatting | bytes 7340032
  15.9 2.2 convert.1
  18.2 8.7 %fusion.1 = f32[8,57344]{1,0:T(8,128)} fusion(f32[16,8]{1,0:T(8,128)S(1)} %stack.167, f32[16,57344]{1,0:T(8,128)} %bitcast.505, f32[2,8,448,128]{3,2,1,0:T(8,128)} %convert.1), kind=kOutput, calls=%fused_computation.3 | convolution fusion | flops 88997888 | bytes 9175552 | tf_op jit(solution)/shard_map/dot_general | solution.py:72
  26.9 1.8 concatenate.9
  28.7 2.3 %copy.183 = f32[56,64,128]{2,0,1:T(8,128)} copy(f32[56,64,128]{2,1,0:T(8,128)S(1)} %concatenate.9) | data formatting | bytes 3670016 | tf_op jit(solution)/shard_map/concatenate | solution.py:77
  33.5 1.2 fusion.3
  35.1 83.3 %all_to_all.18 = f32[100,64,128]{2,0,1:T(8,128)S(1)} all-to-all(f32[100,64,128]{2,0,1:T(8,128)S(1)} %pad_maximum_fusion), channel_id=1, replica_groups=mesh['date'=4,'pix'=8] {'pix'}, dimensions={1} | all-to-all | bytes 6553600 | tf_op jit(solution)/shard_map/all_to_all | solution.py:81
  118.4 2.3 copy.245
  120.7 44.1 %reduce-scatter.2.cloned.1.call-done = f32[100,8,256]{2,1,0:T(8,128)} async-done(((f32[100,8,1024]{2,1,0:T(8,128)}), f32[100,8,256]{2,1,0:T(8,128)}) %reduce-scatter.2.cloned.1.call-update) | async-done | bytes 819216 | tf_op jit(solution)/shard_map/reduce_scatter | solution.py:82
  164.8 0.9 add_bitcast_fusion
  165.7 1.5 slice_reduce_fusion
  167.6 0.9 fusion.104
  168.6 0.8 rsqrt_multiply_fusion.39
  169.4 0.9 rsqrt_multiply_fusion.28
  170.3 0.9 rsqrt_multiply_fusion.26
  171.1 0.9 rsqrt_multiply_fusion.27
  173.5 0.8 subtract_sqrt_fusion.7
  174.3 0.8 rsqrt_multiply_fusion.10
  175.1 0.8 subtract_sqrt_fusion.6
  178.0 0.9 fusion.93
  179.2 0.8 copy.186
  180.0 39.5 %all-reduce = (f32[7]{0:T(128)S(1)}, f32[]{:T(128)}) all-reduce(f32[7]{0:T(128)S(1)} %get-tuple-element.12, f32[]{:T(128)} %get-tuple-element.192), channel_id=1, replica_groups=mesh['date'=4,'pix'=8] {'date','pix'}, use_global_device_ids=true, to_apply=%region_5.0 | all-reduce | flops 8 | bytes 64 | tf_op jit(solution)/shard_map/psum | solution.py:98
  (138 shorter events, 9.7 us)
Async XLA Ops:
  7.2 3.5 %copy-start.3 = (s32[16]{0:T(128)S(1)}, s32[16]{0:T(128)}, u32[]{:S(2)}) copy-start(s32[16]{0:T(128)} %param.5) | copy-start | bytes 196
  7.2 157.6 %reduce-scatter.2.cloned.1.call-start = ((), (), s32[]{:S(2)}) async-start(), calls=%async_computation.2 | async-start | bytes 4096000 | tf_op jit(solution)/shard_map/reduce_scatter | solution.py:82
  12.0 3.9 %copy-start.1 = (bf16[16,7,64,128]{3,2,1,0:T(8,128)(2,1)S(1)}, bf16[16,7,64,128]{3,2,1,0:T(8,128)(2,1)}, u32[]{:S(2)}) copy-start(bf16[16,7,64,128]{3,2,1,0:T(8,128)(2,1)} %param.3) | copy-start | bytes 5505028
  31.0 3.7 %copy-start.2 = (f32[56,64,128]{2,0,1:T(8,128)S(1)}, f32[56,64,128]{2,0,1:T(8,128)}, u32[]{:S(2)}) copy-start(f32[56,64,128]{2,0,1:T(8,128)} %copy.183) | copy-start | bytes 5505028
  164.8 11.1 %copy-start = (f32[100,8,256]{2,1,0:T(8,128)S(1)}, f32[100,8,256]{2,1,0:T(8,128)}, u32[]{:S(2)}) copy-start(f32[100,8,256]{2,1,0:T(8,128)} %reduce-scatter.2.cloned.1.call-done) | copy-start | bytes 2457604
  176.3 1.4 slice-start
Sparse Core Ops, SparseCore 0:
  120.8 43.9 reduce-scatter.1
where the time goes:
time: 229 us; the launch traced here: 228 us
  blocking collectives  123 us (54%)
  waiting for transfers between devices  44.1 us (19%)
  other arithmetic  19.6 us (9%)
  local copies, waits for them, and re-layouts  16.5 us (7%)
  between operations  14.7 us (6%)
  matrix products  9.93 us (4%)
    all_to_all x1, blocking collectives, local(): lax.all_to_all(stacked, 'pix', split_axis=1, concat_axis=2, tiled=True)  83.3 us
    reduce_scatter x1, waiting for transfers between devices, local(): summed = lax.psum_scatter(spread, 'date', scatter_dimension=2, tiled=True)  44.1 us
    psum x1, blocking collectives, local(): lax.psum((jnp.sum(ssr, 1), jnp.sum(wsum)), ('date', 'pix'))  39.5 us
    dot_general x1, matrix products, local(): jnp.dot(design.T, weighted.reshape(local_dates, bands * arrive_pixels), p...  8.69 us
    div x14, other arithmetic, chol_solve(): lower[first, second] = total / lower[second, second]  5.87 us
    unnamed x54, local copies, waits for them, and re-layouts  5.3 us
  transfers between devices with their start and end apart: 1, of which 1 were waited for; matrix products, arithmetic and copies ran while one was open for 0% of the time, Pallas kernels for 0%

commit v1 on v0

--- a/solution.py
+++ b/solution.py
@@ -60,6 +60,12 @@
 
 
 def local(stack, quality, days):
+
+    def rings_connect(piece_in, comm_axis, bus_axis):
+        for u in (comm_axis, bus_axis):
+            piece_in = lax.psum(piece_in, u)
+        return piece_in
+
     high = lax.Precision.HIGHEST
     bands = stack.shape[1]
     local_dates, all_rows, arrive_cols = (stack.shape[0], stack.shape[2], stack.shape[3])
@@ -95,7 +101,7 @@
                 ssr
                 + gram[pair_number(first, second)][None, :] * coef_flat[first] * coef_flat[second]
             )
-    total_ssr, total_weight = lax.psum((jnp.sum(ssr, 1), jnp.sum(wsum)), ("date", "pix"))
+    total_ssr, total_weight = rings_connect((jnp.sum(ssr, 1), jnp.sum(wsum)), "date", "pix")
     sigma2 = total_ssr / total_weight
     score = jnp.sqrt(ssr / (wsum[None, :] + 1.0)) / jnp.sqrt(sigma2)[:, None]
     coef = jnp.transpose(coef_flat.reshape(8, bands, row_count, col_count), (1, 0, 2, 3))

time: 229 us -> 214 us (0.934)
  blocking collectives: 123 us -> 108 us
    psum x1 -> x2, blocking collectives: 39.5 us -> 24.3 us  [rings_connect(): piece_in = lax.psum(piece_in, u)]
where the time goes in v1:
time: 214 us; the launch traced here: 213 us
  blocking collectives  108 us (50%)
  waiting for transfers between devices  44.1 us (21%)
  other arithmetic  19.6 us (9%)
  local copies, waits for them, and re-layouts  16.5 us (8%)
  between operations  14.7 us (7%)
  matrix products  9.93 us (5%)
    all_to_all x1, blocking collectives, local(): lax.all_to_all(stacked, 'pix', split_axis=1, concat_axis=2, tiled=True)  83.3 us
    reduce_scatter x1, waiting for transfers between devices, local(): summed = lax.psum_scatter(spread, 'date', scatter_dimension=2, tiled=True)  44.1 us
    psum x2, blocking collectives, rings_connect(): piece_in = lax.psum(piece_in, u)  24.3 us
    dot_general x1, matrix products, local(): jnp.dot(design.T, weighted.reshape(local_dates, bands * arrive_pixels), p...  8.69 us
    div x14, other arithmetic, chol_solve(): lower[first, second] = total / lower[second, second]  5.87 us
    unnamed x54, local copies, waits for them, and re-layouts  5.31 us
  transfers between devices with their start and end apart: 1, of which 1 were waited for; matrix products, arithmetic and copies ran while one was open for 0% of the time, Pallas kernels for 0%

profile of v1, /device:TPU:0, one launch (start us, length us, event | category | flops | bytes accessed | tf_op | source)
XLA Modules:
  0.0 212.5 jit_solution(11609800216391630051)
XLA Ops:
  7.2 1.2 fusion.103
  8.5 2.0 fusion
  12.0 3.9 %copy.189 = f32[2,8,7,8192]{3,1,2,0:T(8,128)} copy(f32[2,8,7,8192]{3,2,1,0:T(8,128)S(1)} %bitcast.504) | data formatting | bytes 7340032
  16.0 2.2 %convert.1 = f32[2,8,448,128]{3,2,1,0:T(8,128)} convert(bf16[2,8,448,128]{3,2,1,0:T(8,128)(2,1)S(1)} %bitcast.508) | non-fusion elementwise | flops 917504 | bytes 5505024
  18.3 8.7 %fusion.1 = f32[8,57344]{1,0:T(8,128)} fusion(f32[16,8]{1,0:T(8,128)S(1)} %stack.167, f32[16,57344]{1,0:T(8,128)} %bitcast.505, f32[2,8,448,128]{3,2,1,0:T(8,128)} %convert.1), kind=kOutput, calls=%fused_computation.3 | convolution fusion | flops 88997888 | bytes 9175552 | tf_op jit(solution)/shard_map/dot_general | solution.py:78
  26.9 1.8 concatenate.9
  28.7 2.3 %copy.183 = f32[56,64,128]{2,0,1:T(8,128)} copy(f32[56,64,128]{2,1,0:T(8,128)S(1)} %concatenate.9) | data formatting | bytes 3670016 | tf_op jit(solution)/shard_map/concatenate | solution.py:83
  33.5 1.2 fusion.3
  35.1 83.3 %all_to_all.18 = f32[100,64,128]{2,0,1:T(8,128)S(1)} all-to-all(f32[100,64,128]{2,0,1:T(8,128)S(1)} %pad_maximum_fusion), channel_id=1, replica_groups=mesh['date'=4,'pix'=8] {'pix'}, dimensions={1} | all-to-all | bytes 6553600 | tf_op jit(solution)/shard_map/all_to_all | solution.py:87
  118.4 2.3 %copy.245 = f32[100,8,8,128]{3,1,2,0:T(8,128)} copy(f32[100,8,8,128]{3,0,1,2:T(8,128)S(1)} %bitcast.506) | data formatting | bytes 6553600 | tf_op jit(solution)/shard_map/all_to_all | solution.py:87
  120.7 44.1 %reduce-scatter.2.cloned.1.call-done = f32[100,8,256]{2,1,0:T(8,128)} async-done(((f32[100,8,1024]{2,1,0:T(8,128)}), f32[100,8,256]{2,1,0:T(8,128)}) %reduce-scatter.2.cloned.1.call-update) | async-done | bytes 819216 | tf_op jit(solution)/shard_map/reduce_scatter | solution.py:88
  164.8 0.9 add_bitcast_fusion
  165.7 1.5 slice_reduce_fusion
  167.6 0.9 fusion.104
  168.6 0.8 rsqrt_multiply_fusion.39
  169.4 0.9 rsqrt_multiply_fusion.28
  170.3 0.9 rsqrt_multiply_fusion.26
  171.1 0.9 rsqrt_multiply_fusion.27
  173.5 0.8 subtract_sqrt_fusion.7
  175.1 0.8 subtract_sqrt_fusion.6
  178.0 0.9 fusion.93
  179.2 0.8 copy.186
  180.0 9.5 %all-reduce.1 = (f32[7]{0:T(128)S(1)}, f32[]{:T(128)}) all-reduce(f32[7]{0:T(128)S(1)} %get-tuple-element.14, f32[]{:T(128)} %get-tuple-element.194), channel_id=1, replica_groups=mesh['date'=4,'pix'=8] {'date'}, use_global_device_ids=true, to_apply=%region_5.0 | all-reduce | flops 8 | bytes 64 | tf_op jit(solution)/shard_map/psum | solution.py:66
  189.5 14.8 %all-reduce = (f32[7]{0:T(128)S(1)}, f32[]{:T(128)}) all-reduce(f32[7]{0:T(128)S(1)} %get-tuple-element.12, f32[]{:T(128)} %get-tuple-element.13), channel_id=1, replica_groups=mesh['date'=4,'pix'=8] {'pix'}, use_global_device_ids=true, to_apply=%region_6.0 | all-reduce | flops 8 | bytes 64 | tf_op jit(solution)/shard_map/psum | solution.py:66
  (139 shorter events, 10.4 us)
Async XLA Ops:
  7.2 3.5 %copy-start.3 = (s32[16]{0:T(128)S(1)}, s32[16]{0:T(128)}, u32[]{:S(2)}) copy-start(s32[16]{0:T(128)} %param.5) | copy-start | bytes 196
  7.2 157.6 %reduce-scatter.2.cloned.1.call-start = ((), (), s32[]{:S(2)}) async-start(), calls=%async_computation.2 | async-start | bytes 4096000 | tf_op jit(solution)/shard_map/reduce_scatter | solution.py:88
  12.0 3.9 %copy-start.1 = (bf16[16,7,64,128]{3,2,1,0:T(8,128)(2,1)S(1)}, bf16[16,7,64,128]{3,2,1,0:T(8,128)(2,1)}, u32[]{:S(2)}) copy-start(bf16[16,7,64,128]{3,2,1,0:T(8,128)(2,1)} %param.3) | copy-start | bytes 5505028
  31.0 3.7 %copy-start.2 = (f32[56,64,128]{2,0,1:T(8,128)S(1)}, f32[56,64,128]{2,0,1:T(8,128)}, u32[]{:S(2)}) copy-start(f32[56,64,128]{2,0,1:T(8,128)} %copy.183) | copy-start | bytes 5505028
  164.8 11.1 %copy-start = (f32[100,8,256]{2,1,0:T(8,128)S(1)}, f32[100,8,256]{2,1,0:T(8,128)}, u32[]{:S(2)}) copy-start(f32[100,8,256]{2,1,0:T(8,128)} %reduce-scatter.2.cloned.1.call-done) | copy-start | bytes 2457604
  176.3 1.4 slice-start
Sparse Core Ops, SparseCore 0:
  120.8 43.9 reduce-scatter.1
